TPU v7x, 32 devices: a whole 2x2x4 slice. The times are simulated.
32 devices in a mesh: slab: 8 (over z, x), gy: 4 (over y, core).
Axes of the slice: x: 2, y: 2, z: 4, core: 2. Of those that a mesh axis runs over, the one named last changes fastest.
Arguments:
- displacement: float32 [3, 32, 64, 512], P(None, None, 'slab', 'gy'), may hold values from -6 to 6
- previous: float32 [3, 32, 64, 512], P(None, None, 'slab', 'gy'), may hold values from -6 to 6
- shear_coef: float32 [32, 64, 512], P(None, 'slab', 'gy'), may hold values from 0.04 to 0.16
- bulk_coef: float32 [32, 64, 512], P(None, 'slab', 'gy'), may hold values from 0.02 to 0.16
- cell_index: int32 [32768], P(('slab', 'gy')), may hold values from 0 to 32767, as said below
- archetype_id: int32 [32768, 1], P(('slab', 'gy')), may hold values from 0 to 1023; in each aligned block of 1024 rows (0 to 1023, 1024 to 2047, ...) at most 2 rows name the same one
- transition: bfloat16 [1024, 256, 256], P(('slab', 'gy')), may hold values from -1 to 1
- forcing: float32 [1024, 3, 256], P(('slab', 'gy')), may hold values from -3 to 3
Outputs:
- final_field: float32 [3, 32, 64, 512], P(None, None, 'slab', 'gy')
- building_state: float32 [32768, 256], P(('slab', 'gy'))
Inputs may be any that keep to these rules, and one draw needn't show every extreme that they name: `cell_index`: building b's cell has x between s * 8 and s * 8 + 7, where s = (b // 1024) // 4; y is any. `archetype_id`: among the 1024 buildings of one device no archetype appears more than 2 times.
All inputs are finite; a program needn't handle non-finite values.
Results may differ from a plain program's by a relative error of at most 0.0023.
Values sent between devices are 32-bit elements; how exact they have to be, the bound alone decides.
A program may use at most 64 MiB of HBM per device.

v0:
```python
import functools

import jax
import jax.numpy as jnp
from jax import lax
from jax.experimental import pallas as pl
from jax.experimental.pallas import tpu as pltpu
from jax.sharding import PartitionSpec as P

COUPLINGS = 4
EVERY = 5
SUB = 6
CAP = 2
CHUNKS = 2
ARCH_BLOCK = 4
PLANES = 4

A0, A1, A2 = -30.0 / 12.0, 16.0 / 12.0, -1.0 / 12.0
B1, B2 = 8.0 / 12.0, -1.0 / 12.0
DIRECTIONS = ((-1, 0), (1, 0), (0, -1), (0, 1), (-1, -1), (1, -1), (-1, 1), (1, 1))


def second(mid, plus1, minus1, plus2, minus2):
    return A0 * mid + A1 * (plus1 + minus1) + A2 * (plus2 + minus2)


def first(plus1, minus1, plus2, minus2):
    return B1 * (plus1 - minus1) + B2 * (plus2 - minus2)


def grid_kernel(
    steps, every, d_ref, p_ref, sh_ref, bk_ref, f_ref, surf_ref,
    buf, ps, pr, ht, ah, hx, e_ref, s_ref, send, recv,
):
    nz, cx, cy = sh_ref.shape
    slab, gy = lax.axis_index("slab"), lax.axis_index("gy")
    slabs, gys = lax.axis_size("slab"), lax.axis_size("gy")
    blocks = nz // PLANES

    def exists(dx, dy):
        x, y = slab + dx, gy + dy
        return (x >= 0) & (x < slabs) & (y >= 0) & (y < gys)

    buf[...] = jnp.zeros_like(buf)
    pr[...] = jnp.zeros_like(pr)
    ht[...] = jnp.zeros_like(ht)
    e_ref[...] = jnp.zeros_like(e_ref)
    buf[0, :, 2 : nz + 2, 8:16, :] = d_ref[...]
    buf[1, :, 2 : nz + 2, 8:16, :] = p_ref[...]

    barrier = pltpu.get_barrier_semaphore()
    for dx, dy in DIRECTIONS:
        @pl.when(exists(dx, dy))
        def _():
            pl.semaphore_signal(
                barrier, inc=1, device_id=(slab + dx, gy + dy),
                device_id_type=pl.DeviceIdType.MESH,
            )
    spans = [
        1 + jnp.where(at > 0, 1, 0) + jnp.where(at < size - 1, 1, 0)
        for at, size in ((slab, slabs), (gy, gys))
    ]
    pl.semaphore_wait(barrier, spans[0] * spans[1] - 1)

    def copy_of(k, par):
        dx, dy = DIRECTIONS[k]
        mine = slice(0, 2) if dx < 0 else slice(cx - 2, cx)
        theirs = slice(16, 18) if dx < 0 else slice(6, 8)
        if dy == 0:
            src = buf.at[par, :, 2 : nz + 2, mine.start + 8 : mine.stop + 8, :]
            dst = buf.at[par, :, 2 : nz + 2, theirs, :]
        elif dx == 0:
            src = ps.at[par]
            dst = pr.at[par, 1 if dy < 0 else 0, :, 8:16, :]
        else:
            src = ps.at[par, :, mine, :]
            dst = pr.at[par, 1 if dy < 0 else 0, :, theirs, :]
        return pltpu.make_async_remote_copy(
            src_ref=src, dst_ref=dst, send_sem=send.at[par, k], recv_sem=recv.at[par, k],
            device_id=(slab + dx, gy + dy), device_id_type=pl.DeviceIdType.MESH,
        )

    lane3 = lax.broadcasted_iota(jnp.int32, (PLANES, cx, cy), 2)
    lane = lax.broadcasted_iota(jnp.int32, (cx, cy), 1)
    row3 = lax.broadcasted_iota(jnp.int32, (PLANES, cx, cy), 1)
    row = lax.broadcasted_iota(jnp.int32, (cx, cy), 0)

    def along_y(core, halo):
        return (
            pltpu.roll(jnp.where(lane3 < 1, halo, core), cy - 1, 2),
            pltpu.roll(jnp.where(lane3 >= cy - 1, halo, core), 1, 2),
            pltpu.roll(jnp.where(lane3 < 2, halo, core), cy - 2, 2),
            pltpu.roll(jnp.where(lane3 >= cy - 2, halo, core), 2, 2),
        )

    def step(n, carry):
        par = lax.rem(n, 2)
        new = 1 - par

        for k in range(2):
            @pl.when(exists(*DIRECTIONS[k]))
            def _():
                copy_of(k, par).start()

        for c in range(3):
            packed = jnp.zeros((cx, cy), jnp.float32)
            for d in range(nz):
                turned = pltpu.roll(buf[par, c, d + 2, 8:16, :], 2 + 4 * d, 1) if (2 + 4 * d) % cy else buf[par, c, d + 2, 8:16, :]
                packed = jnp.where((lane >= 4 * d) & (lane < 4 * d + 4), turned, packed)
            ps[par, c] = packed

        for k in range(2, 8):
            @pl.when(exists(*DIRECTIONS[k]))
            def _():
                copy_of(k, par).start()

        for c in range(3):
            buf[par, c, 0, 8:16, :] = buf[par, c, 4, 8:16, :]
            buf[par, c, 1, 8:16, :] = buf[par, c, 3, 8:16, :]

        for k in range(8):
            @pl.when(exists(*DIRECTIONS[k]))
            def _():
                copy_of(k, par).wait_send()
        for k in range(8):
            dx, dy = DIRECTIONS[k]
            @pl.when(exists(-dx, -dy))
            def _():
                copy_of(k, par).wait_recv()

        for lo in (0, 16):
            buf[par, 2, 0, lo : lo + 8, :] = buf[par, 2, 4, lo : lo + 8, :]
            buf[par, 2, 1, lo : lo + 8, :] = buf[par, 2, 3, lo : lo + 8, :]

        from_left = lax.rem(lane, 4) < 2

        def joined(c, lo):
            return jnp.where(from_left, pr[par, 0, c, lo : lo + 8, :], pr[par, 1, c, lo : lo + 8, :])

        g = [joined(c, 8) for c in range(3)]
        g_y = jnp.where(row < 4, joined(1, 16), joined(1, 0))
        g_x = jnp.where(row < 4, joined(0, 16), joined(0, 0))
        a_g = first(
            pltpu.roll(jnp.where(row < 1, g_x, g[0]), cx - 1, 0),
            pltpu.roll(jnp.where(row >= cx - 1, g_x, g[0]), 1, 0),
            pltpu.roll(jnp.where(row < 2, g_x, g[0]), cx - 2, 0),
            pltpu.roll(jnp.where(row >= cx - 2, g_x, g[0]), 2, 0),
        )
        for d in range(nz):
            back = (cy - 4 * d - 2) % cy
            for c in range(3):
                ht[c, d + 2] = pltpu.roll(g[c], back, 1)
            ah[d] = pltpu.roll(a_g, back, 1)
            hx[d] = pltpu.roll(g_y, back, 1)
        ht[2, 0] = ht[2, 4]
        ht[2, 1] = ht[2, 3]

        def u(c, d, shift, lo):
            return buf[par, c, pl.ds(d + 2 + shift, PLANES), lo : lo + 8, :]

        def prepare(b, carry):
            d = b * PLANES
            a = first(u(0, d, 0, 9), u(0, d, 0, 7), u(0, d, 0, 10), u(0, d, 0, 6))
            bb = first(*along_y(u(1, d, 0, 8), ht[1, pl.ds(d + 2, PLANES)]))
            e_ref[pl.ds(d + 2, PLANES)] = a + bb
            cc = first(u(2, d, 1, 8), u(2, d, -1, 8), u(2, d, 2, 8), u(2, d, -2, 8))
            s_ref[pl.ds(d, PLANES), 8:16, :] = bb + cc

            def mixed(comp, shift):
                return jnp.where(row3 < 4, u(comp, d, shift, 16), u(comp, d, shift, 0))

            s_halo = first(*along_y(mixed(1, 0), hx[pl.ds(d, PLANES)])) + first(
                mixed(2, 1), mixed(2, -1), mixed(2, 2), mixed(2, -2)
            )
            s_ref[pl.ds(d, PLANES), 0:8, :] = s_halo
            s_ref[pl.ds(d, PLANES), 16:24, :] = s_halo
            return carry

        lax.fori_loop(0, blocks, prepare, 0)
        e_ref[0] = e_ref[4]
        e_ref[1] = e_ref[3]

        def advance(b, carry):
            d = b * PLANES
            sh = sh_ref[pl.ds(d, PLANES)]
            bk = bk_ref[pl.ds(d, PLANES)]

            def h(c, shift):
                return ht[c, pl.ds(d + 2 + shift, PLANES)]

            def s(lo):
                return s_ref[pl.ds(d, PLANES), lo : lo + 8, :]

            def e(shift):
                return e_ref[pl.ds(d + 2 + shift, PLANES)]

            a = first(u(0, d, 0, 9), u(0, d, 0, 7), u(0, d, 0, 10), u(0, d, 0, 6))
            cc = first(u(2, d, 1, 8), u(2, d, -1, 8), u(2, d, 2, 8), u(2, d, -2, 8))
            c_halo = first(h(2, 1), h(2, -1), h(2, 2), h(2, -2))
            t_halo = ah[pl.ds(d, PLANES)] + c_halo
            for c in range(3):
                mid = u(c, d, 0, 8)
                along = (
                    second(mid, u(c, d, 0, 9), u(c, d, 0, 7), u(c, d, 0, 10), u(c, d, 0, 6)),
                    second(mid, *along_y(mid, h(c, 0))),
                    second(mid, u(c, d, 1, 8), u(c, d, -1, 8), u(c, d, 2, 8), u(c, d, -2, 8)),
                )
                if c == 0:
                    cross = first(s(9), s(7), s(10), s(6))
                elif c == 1:
                    cross = first(*along_y(a + cc, t_halo))
                else:
                    cross = first(e(1), e(-1), e(2), e(-2))
                acc = sh * (along[0] + along[1] + along[2]) + bk * (along[c] + cross)
                place = (new, c, pl.ds(d + 2, PLANES), slice(8, 16), slice(None))
                buf[place] = 2.0 * mid - buf[place] + acc
            return carry

        lax.fori_loop(0, blocks, advance, 0)
        surf_ref[lax.div(n, every)] = buf[new, :, 2, 8:16, :]
        return carry

    lax.fori_loop(0, steps, step, 0)
    f_ref[...] = buf[steps % 2, :, 2 : nz + 2, 8:16, :]


def run_grid(displacement, previous, shear_coef, bulk_coef):
    _, nz, cx, cy = displacement.shape
    vmem = pl.BlockSpec(memory_space=pltpu.VMEM)
    f32 = jnp.float32
    return pl.pallas_call(
        functools.partial(grid_kernel, COUPLINGS * EVERY, EVERY),
        out_shape=(
            jax.ShapeDtypeStruct(displacement.shape, f32),
            jax.ShapeDtypeStruct((COUPLINGS, 3, cx, cy), f32),
        ),
        in_specs=[vmem] * 4,
        out_specs=(vmem, vmem),
        scratch_shapes=[
            pltpu.VMEM((2, 3, nz + 4, cx + 16, cy), f32),
            pltpu.VMEM((2, 3, cx, cy), f32),
            pltpu.VMEM((2, 2, 3, cx + 16, cy), f32),
            pltpu.VMEM((3, nz + 4, cx, cy), f32),
            pltpu.VMEM((nz, cx, cy), f32),
            pltpu.VMEM((nz, cx, cy), f32),
            pltpu.VMEM((nz + 4, cx, cy), f32),
            pltpu.VMEM((nz, cx + 16, cy), f32),
            pltpu.SemaphoreType.DMA((2, 8)),
            pltpu.SemaphoreType.DMA((2, 8)),
        ],
        compiler_params=pltpu.CompilerParams(
            collective_id=0, has_side_effects=True, vmem_limit_bytes=32 * 1024 * 1024
        ),
    )(displacement, previous, shear_coef, bulk_coef)


def building_kernel(couplings, sub, m_ref, f_ref, t_ref, o_ref):
    block, rows, _ = m_ref.shape
    width = t_ref.shape[1]
    states = [jnp.zeros((rows, width), jnp.float32) for _ in range(block)]
    for moment in range(couplings):
        drives = []
        for i in range(block):
            drive = m_ref[i, :, 3 * moment : 3 * moment + 1] * f_ref[i, 0:1, :]
            drive = drive + m_ref[i, :, 3 * moment + 1 : 3 * moment + 2] * f_ref[i, 1:2, :]
            drive = drive + m_ref[i, :, 3 * moment + 2 : 3 * moment + 3] * f_ref[i, 2:3, :]
            drives.append(drive)
        for inner in range(sub):
            for i in range(block):
                if moment == 0 and inner == 0:
                    states[i] = drives[i]
                else:
                    states[i] = drives[i] + lax.dot_general(
                        states[i].astype(jnp.bfloat16), t_ref[i],
                        (((1,), (1,)), ((), ())), preferred_element_type=jnp.float32,
                    )
    for i in range(block):
        o_ref[:, CAP * i : CAP * (i + 1), :] = states[i].reshape(rows // CAP, CAP, width)


def run_buildings(motion, forcing, transition, start, kinds):
    rows, parts = motion.shape[1], motion.shape[2]
    width = transition.shape[1]
    first_block = start // ARCH_BLOCK
    return pl.pallas_call(
        functools.partial(building_kernel, COUPLINGS, SUB),
        grid=(kinds // ARCH_BLOCK,),
        out_shape=jax.ShapeDtypeStruct((rows // CAP, kinds * CAP, width), jnp.float32),
        in_specs=[
            pl.BlockSpec((ARCH_BLOCK, rows, parts), lambda i: (i + first_block, 0, 0)),
            pl.BlockSpec((ARCH_BLOCK, 3, width), lambda i: (i + first_block, 0, 0)),
            pl.BlockSpec((ARCH_BLOCK, width, width), lambda i: (i + first_block, 0, 0)),
        ],
        out_specs=pl.BlockSpec((rows // CAP, ARCH_BLOCK * CAP, width), lambda i: (0, i, 0)),
        cost_estimate=pl.CostEstimate(
            flops=2 * kinds * rows * width * width * COUPLINGS * SUB,
            bytes_accessed=2 * kinds * width * width + 4 * kinds * rows * width,
            transcendentals=0,
        ),
    )(motion, forcing, transition)


def per_device(
    displacement, previous, shear_coef, bulk_coef, cell_index, archetype_id, transition, forcing
):
    groups = lax.axis_size("slab") * lax.axis_size("gy")
    arch_local = transition.shape[0]
    width = transition.shape[1]
    slots_dev = arch_local * CAP
    count = cell_index.shape[0]
    kinds = archetype_id[:, 0]
    order = jnp.arange(count, dtype=jnp.int32)
    earlier = (kinds[:, None] == kinds[None, :]) & (order[None, :] < order[:, None])
    position = jnp.sum(earlier.astype(jnp.int32), axis=1)
    slot_index = kinds * CAP + position
    cells = displacement.shape[2] * displacement.shape[3] * lax.axis_size("gy")
    local_cell = cell_index - lax.axis_index("slab") * cells
    slots = jnp.arange(groups * slots_dev, dtype=jnp.int32)
    slot_cell = jnp.sum(
        jnp.where(slot_index[None, :] == slots[:, None], local_cell[None, :], 0), axis=1
    )

    field, surface = run_grid(displacement, previous, shear_coef, bulk_coef)

    parts = 3 * COUPLINGS
    surface = lax.all_gather(surface, "gy", axis=3, tiled=True)
    table = surface.reshape(parts, cells).T
    motion = jnp.take(table, slot_cell, axis=0, mode="clip")
    motion = motion.reshape(groups, slots_dev, parts).transpose(0, 2, 1)
    pushed = lax.all_to_all(motion, ("slab", "gy"), split_axis=0, concat_axis=0, tiled=True)
    pushed = pushed.reshape(groups, parts, arch_local, CAP).transpose(2, 0, 3, 1)
    pushed = pushed.reshape(arch_local, groups * CAP, parts)

    share = arch_local // CHUNKS
    pieces = []
    for chunk in range(CHUNKS):
        states = run_buildings(pushed, forcing, transition, chunk * share, share)
        returned = lax.all_to_all(
            states, ("slab", "gy"), split_axis=0, concat_axis=0, tiled=True
        )
        pieces.append(returned.reshape(groups * share * CAP, width))
    owner, kind = kinds // arch_local, kinds % arch_local
    chunk_of = kind // share
    home = chunk_of * (groups * share * CAP) + owner * (share * CAP)
    home = home + (kind - chunk_of * share) * CAP + position
    home_state = jnp.take(jnp.concatenate(pieces, axis=0), home, axis=0, mode="clip")
    return (field, home_state)


def solution(mesh):
    in_specs = (
        P(None, None, "slab", "gy"),
        P(None, None, "slab", "gy"),
        P(None, "slab", "gy"),
        P(None, "slab", "gy"),
        P(("slab", "gy")),
        P(("slab", "gy"), None),
        P(("slab", "gy"), None, None),
        P(("slab", "gy"), None, None),
    )
    out_specs = (P(None, None, "slab", "gy"), P(("slab", "gy"), None))
    return jax.shard_map(
        per_device, mesh=mesh, in_specs=in_specs, out_specs=out_specs, check_vma=False
    )
```

profile of v0, /device:TPU:0, one launch (start us, length us, event | category | flops | bytes accessed | tf_op | source)
XLA Modules:
  0.0 307.9 jit_solution(2782993050878474944)
XLA Ops:
  0.6 1.3 convert_reduce_fusion
  2.6 0.9 select_reduce_fusion
  3.6 1.0 copy-done
  4.6 1.0 copy-done.1
  5.6 0.9 copy-done.2
  6.5 0.9 copy-done.3
  7.4 186.6 %shard_map.95 = (f32[3,32,8,128]{3,2,1,0:T(8,128)S(1)}, f32[4,3,8,128]{3,2,1,0:T(8,128)S(1)}) custom-call(f32[3,32,8,128]{3,2,1,0:T(8,128)S(1)} %copy-done, f32[3,32,8,128]{3,2,1,0:T(8,128)S(1)} %copy-done.1, f32[32,8,128]{2,1,0:T(8,128)S(1)} %copy-done.2, f32[32,8,128]{2,1,0:T(8,128)S(1)} %copy-done.3), custom_call_target="tpu_custom_call" | custom-call | tf_op jit(solution)/shard_map/pallas_call | solution.py:231
  194.0 5.6 %all_gather.3 = f32[4,3,8,512]{3,2,1,0:T(8,128)S(1)} all-gather(f32[4,3,8,128]{3,2,1,0:T(8,128)S(1)} %get-tuple-element.5), channel_id=1, replica_groups=mesh['slab'=8,'gy'=4] {'gy'}, dimensions={3}, use_global_device_ids=true | all-gather | bytes 245760 | tf_op jit(solution)/shard_map/all_gather | solution.py:326
  200.4 5.5 %gather_fusion = f32[2048,12]{1,0:T(8,128)S(1)} fusion(f32[4096,12]{1,0:T(8,128)S(1)} %bitcast.16, s32[2048]{0:T(1024)S(1)} %broadcast_clamp_fusion), kind=kCustom, calls=%fused_computation | custom fusion | bytes 204800 | tf_op jit(solution)/shard_map/jit(_take)/gather | solution.py:328
  206.3 0.8 reshape.56
  207.1 6.7 %all-to-all-start = ((f32[32,1,768]{2,1,0:T(1,128)}), f32[32,1,768]{2,1,0:T(1,128)S(1)}, u32[]{:S(2)}, u32[]{:S(2)}) async-start(f32[32,1,768]{2,1,0:T(1,128)} %reshape.56), calls=%async_computation | async-start | bytes 196608 | tf_op jit(solution)/shard_map/all_to_all | solution.py:330
  213.8 1.6 copy.28.f_ref
  215.4 6.2 %all-to-all-done = f32[32,1,768]{2,1,0:T(1,128)S(1)} async-done(((f32[32,1,768]{2,1,0:T(1,128)}), f32[32,1,768]{2,1,0:T(1,128)S(1)}, u32[]{:S(2)}, u32[]{:S(2)}) %all-to-all-start) | async-done | bytes 98336 | tf_op jit(solution)/shard_map/all_to_all | solution.py:330
  222.1 0.9 reduce
  223.3 1.4 copy.27
  224.7 16.9 %shard_map.96 = f32[32,32,256]{2,1,0:T(8,128)} custom-call(f32[32,64,12]{2,1,0:T(8,128)} %bitcast.23, f32[32,3,256]{2,1,0:T(4,128)} %copy.28.f_ref, bf16[32,256,256]{2,1,0:T(8,128)(2,1)} %t_ref.3), custom_call_target="tpu_custom_call" | custom-call | flops 3221225472 | bytes 3145728 | tf_op jit(solution)/shard_map/pallas_call | solution.py:285
  241.5 2.6 all-to-all-start.1
  244.2 16.9 %shard_map.97 = f32[32,32,256]{2,1,0:T(8,128)} custom-call(f32[32,64,12]{2,1,0:T(8,128)} %bitcast.24, f32[32,3,256]{2,1,0:T(4,128)} %copy.28.f_ref, bf16[32,256,256]{2,1,0:T(8,128)(2,1)} %t_ref.3), custom_call_target="tpu_custom_call" | custom-call | flops 3221225472 | bytes 3145728 | tf_op jit(solution)/shard_map/pallas_call | solution.py:285
  261.1 9.3 %all-to-all-done.1 = f32[32,32,256]{2,1,0:T(8,128)S(1)} async-done(((f32[32,32,256]{2,1,0:T(8,128)}), f32[32,32,256]{2,1,0:T(8,128)S(1)}, u32[]{:S(2)}, u32[]{:S(2)}) %all-to-all-start.1) | async-done | bytes 1048608 | tf_op jit(solution)/shard_map/all_to_all | solution.py:338
  270.4 3.5 %all-to-all-start.2 = ((f32[32,32,256]{2,1,0:T(8,128)}), f32[32,32,256]{2,1,0:T(8,128)S(1)}, u32[]{:S(2)}, u32[]{:S(2)}) async-start(f32[32,32,256]{2,1,0:T(8,128)} %shard_map.97), calls=%async_computation.2 | async-start | bytes 2097152 | tf_op jit(solution)/shard_map/all_to_all | solution.py:338
  274.0 26.1 %all-to-all-done.2 = f32[32,32,256]{2,1,0:T(8,128)S(1)} async-done(((f32[32,32,256]{2,1,0:T(8,128)}), f32[32,32,256]{2,1,0:T(8,128)S(1)}, u32[]{:S(2)}, u32[]{:S(2)}) %all-to-all-start.2) | async-done | bytes 1048608 | tf_op jit(solution)/shard_map/all_to_all | solution.py:338
  300.1 1.0 copy-done.4
  301.1 1.4 pad_maximum_fusion
  302.5 4.7 %gather_fusion.1 = f32[1024,256]{1,0:T(8,128)} fusion(f32[2048,256]{1,0:T(8,128)S(1)} %pad_maximum_fusion, s32[1024]{0:T(1024)S(1)} %broadcast_clamp_fusion.1), kind=kCustom, calls=%fused_computation.1 | custom fusion | bytes 2101248 | tf_op jit(solution)/shard_map/jit(_take)/gather | solution.py:346
  (19 shorter events, 3.5 us)
Async XLA Ops:
  3.6 1.0 copy-start
  4.6 1.0 copy-start.1
  5.6 0.9 copy-start.2
  6.5 0.9 copy-start.3
  207.1 14.5 %all-to-all-start = ((f32[32,1,768]{2,1,0:T(1,128)}), f32[32,1,768]{2,1,0:T(1,128)S(1)}, u32[]{:S(2)}, u32[]{:S(2)}) async-start(f32[32,1,768]{2,1,0:T(1,128)} %reshape.56), calls=%async_computation | async-start | bytes 196608 | tf_op jit(solution)/shard_map/all_to_all | solution.py:330
  241.5 28.8 %all-to-all-start.1 = ((f32[32,32,256]{2,1,0:T(8,128)}), f32[32,32,256]{2,1,0:T(8,128)S(1)}, u32[]{:S(2)}, u32[]{:S(2)}) async-start(f32[32,32,256]{2,1,0:T(8,128)} %shard_map.96), calls=%async_computation.1 | async-start | bytes 2097152 | tf_op jit(solution)/shard_map/all_to_all | solution.py:338
  244.2 29.7 %copy-start.5 = (s32[1024,1]{0,1:T(1,128)S(1)}, s32[1024,1]{0,1:T(1,128)}, u32[]{:S(2)}) copy-start(s32[1024,1]{0,1:T(1,128)} %param.13) | copy-start | bytes 12292
  270.4 29.8 %all-to-all-start.2 = ((f32[32,32,256]{2,1,0:T(8,128)}), f32[32,32,256]{2,1,0:T(8,128)S(1)}, u32[]{:S(2)}, u32[]{:S(2)}) async-start(f32[32,32,256]{2,1,0:T(8,128)} %shard_map.97), calls=%async_computation.2 | async-start | bytes 2097152 | tf_op jit(solution)/shard_map/all_to_all | solution.py:338
  300.1 1.0 copy-start.4
where the time goes:
time: 309 us; the launch traced here: 308 us
  Pallas kernels  220 us (71%)
  waiting for transfers between devices  41.6 us (13%)
  local copies, waits for them, and re-layouts  21.5 us (7%)
  starting transfers between devices  12.9 us (4%)
  blocking collectives  5.6 us (2%)
  other arithmetic  5.23 us (2%)
    pallas_call x1, Pallas kernels, run_grid(): pl.pallas_call(functools.partial(grid_kernel, COUPLINGS * EVERY, EVERY),...  187 us
    all_to_all x2, waiting for transfers between devices, per_device(): lax.all_to_all(states, ('slab', 'gy'), split_axis=0, concat_axis=0, tiled...  35.4 us
    pallas_call x2, Pallas kernels, run_buildings(): pl.pallas_call(functools.partial(building_kernel, COUPLINGS, SUB), grid=(...  33.7 us
    unnamed x18, local copies, waits for them, and re-layouts  8.21 us
    all_to_all x1, starting transfers between devices, per_device(): lax.all_to_all(motion, ('slab', 'gy'), split_axis=0, concat_axis=0, tiled...  6.73 us
    all_to_all x2, starting transfers between devices, per_device(): lax.all_to_all(states, ('slab', 'gy'), split_axis=0, concat_axis=0, tiled...  6.18 us
  transfers between devices with their start and end apart: 3, of which 3 were waited for; matrix products, arithmetic and copies ran while one was open for 1% of the time, Pallas kernels for 5%

commit v1 on v0

v1 whole, which is shorter than its diff:
```python
import functools

import jax
import jax.numpy as jnp
from jax import lax
from jax.experimental import pallas as pl
from jax.experimental.pallas import tpu as pltpu
from jax.sharding import PartitionSpec as P

COUPLINGS = 4
EVERY = 5
SUB = 6
UNIT = 8
EARLY = 5
CHUNK = 4
PLANES = 1
SCALE = 2.0 ** 60

A0, A1, A2 = -30.0 / 12.0, 16.0 / 12.0, -1.0 / 12.0
B1, B2 = 8.0 / 12.0, -1.0 / 12.0
DIRECTIONS = ((-1, 0), (1, 0), (0, -1), (0, 1), (-1, -1), (1, -1), (-1, 1), (1, 1))
MESH = pl.DeviceIdType.MESH


def first(plus1, minus1, plus2, minus2):
    return B1 * (plus1 - minus1) + B2 * (plus2 - minus2)


def city_kernel(
    d_hbm, p_hbm, sh_hbm, bk_hbm, cell_ref, kind_ref, t_hbm, f_hbm,
    f_ref, o_ref,
    raw, t_ref, force, sbuf, buf, sh_ref, bk_ref, ps, pr, gx, ht, th, hx, e_ref, s_ref, q_ref,
    vs, g_all, surf, hot, hotx, lhs, mot, fold,
    load_sem, give_send, give_recv, x_send, x_recv, y_send, y_recv,
    near_send, near_recv, hop_send, hop_recv, surf_send, surf_recv, back_send, back_recv,
):
    f32, bf16 = jnp.float32, jnp.bfloat16
    steps = COUPLINGS * EVERY
    cx, cy = sh_hbm.shape[1], sh_hbm.shape[2]
    nz = sh_hbm.shape[0]
    nr = nz // 2
    half = cy // 2
    rows = 2 * cx
    lo, hi = cx, cx + rows
    arch, width = t_hbm.shape[0], t_hbm.shape[1]
    count = kind_ref.shape[0]
    slab, gy = lax.axis_index("slab"), lax.axis_index("gy")
    slabs, gys = lax.axis_size("slab"), lax.axis_size("gy")
    pairs, pieces = slabs // 2, 2 * gys
    k, a = lax.div(slab, 2), lax.rem(slab, 2)
    hsel = lax.rem(a + gy, 2)
    piece = 2 * gy + hsel
    yb, cb = lax.div(gy, 2), lax.rem(gy, 2)
    chunks = nr // CHUNK
    groups = arch // UNIT
    units = groups * COUPLINGS

    def exists(dx, dy):
        x, y = k + dx, piece + dy
        return (x >= 0) & (x < pairs) & (y >= 0) & (y < pieces)

    def target(dx, dy):
        if dy == 0:
            return (2 * (k + dx) + a, gy)
        inner = (hsel == 0) if dy > 0 else (hsel == 1)
        return (2 * (k + dx) + jnp.where(inner, 1 - a, a), jnp.where(inner, gy, gy + dy))

    mate = (2 * k + 1 - a, gy)

    def load(i, src, dst):
        return pltpu.make_async_copy(src, dst, load_sem.at[i])

    loads = [
        load(0, d_hbm, raw.at[0:3]),
        load(1, p_hbm, raw.at[3:6]),
        load(2, sh_hbm, raw.at[6]),
        load(3, bk_hbm, raw.at[7]),
        load(4, t_hbm, t_ref),
        load(5, f_hbm, force),
    ]
    for one in loads:
        one.start()

    zero_tile = jnp.zeros((2, 3, nr + 4, cx, cy), f32)
    buf[:, :, :, 0:lo, :] = zero_tile
    buf[:, :, :, hi : hi + cx, :] = zero_tile
    pr[...] = jnp.zeros_like(pr)
    vs[...] = jnp.zeros_like(vs)
    g_rows = 2 * 3
    mot[...] = jnp.zeros_like(mot)

    barrier = pltpu.get_barrier_semaphore()

    def greet(device):
        pl.semaphore_signal(barrier, inc=1, device_id=device, device_id_type=MESH)

    def row_mates():
        for da in range(2):
            for dg in range(gys):
                if da or dg:
                    yield da, dg, (2 * k + lax.rem(a + da, 2), lax.rem(gy + dg, gys))

    for _, _, device in row_mates():
        greet(device)
    for dk in range(1, pairs):
        greet((2 * lax.rem(k + dk, pairs) + a, gy))
    for dx, dy in DIRECTIONS[4:]:
        @pl.when(exists(dx, dy))
        def _():
            greet(target(dx, dy))
    beside = [
        jnp.where(at > 0, 1, 0) + jnp.where(at < size - 1, 1, 0)
        for at, size in ((k, pairs), (piece, pieces))
    ]

    lane = lax.broadcasted_iota(jnp.int32, (cx, cy), 1)
    row = lax.broadcasted_iota(jnp.int32, (cx, cy), 0)
    left = lane < half

    def folded(near, far, second_half):
        if second_half:
            return jnp.where(left, pltpu.roll(near, half, 1), far)
        return jnp.where(left, near, pltpu.roll(far, half, 1))

    own = pl.ds(pl.multiple_of(cx * a, cx), cx)
    own_buf = pl.ds(pl.multiple_of(lo + cx * a, cx), cx)

    def kept_ref(i, r):
        if i < 3:
            return buf.at[0, i, r + 2, own_buf, :]
        if i < 6:
            return buf.at[1, i - 3, r + 2, own_buf, :]
        return (sh_ref if i == 6 else bk_ref).at[r, own, :]

    def give(i):
        if i < 3:
            dst = buf.at[0, i, 2 : nr + 2, own_buf, :]
        elif i < 6:
            dst = buf.at[1, i - 3, 2 : nr + 2, own_buf, :]
        else:
            dst = (sh_ref if i == 6 else bk_ref).at[:, own, :]
        return pltpu.make_async_remote_copy(
            src_ref=sbuf.at[i], dst_ref=dst, send_sem=give_send.at[i], recv_sem=give_recv.at[i],
            device_id=mate, device_id_type=MESH,
        )

    for i in range(8):
        if i in (0, 3, 6, 7):
            loads[{0: 0, 3: 1, 6: 2, 7: 3}[i]].wait()
        for r in range(nr):
            near, far = raw[i, r], raw[i, nz - 1 - r]
            lower, upper = folded(near, far, False), folded(near, far, True)
            kept_ref(i, r)[...] = jnp.where(hsel == 0, lower, upper)
            sbuf[i, r] = jnp.where(hsel == 0, upper, lower)
        if i == 0:
            corners = beside[0] * beside[1]
            pl.semaphore_wait(barrier, pieces - 1 + pairs - 1 + corners)
        give(i).start()

    ny = gys * cy
    cell = cell_ref[...]
    start = slab * cx
    along_x = jnp.zeros_like(cell)
    for i in range(1, cx):
        along_x = along_x + jnp.where(cell >= (start + i) * ny, 1, 0)
    column = cell - (start + along_x) * ny
    hotx[...] = jnp.where(
        lax.broadcasted_iota(jnp.int32, (cx, count), 0) == along_x, 1.0, 0.0
    )
    for i in range(ny // 128):
        hot[128 * i : 128 * (i + 1), :] = jnp.where(
            lax.broadcasted_iota(jnp.int32, (128, count), 0) + 128 * i == column, 1.0, 0.0
        ).astype(bf16)

    loads[4].wait()
    loads[5].wait()

    def face(dx, par, piece_r):
        mine = lo if dx < 0 else hi - 2
        theirs = hi if dx < 0 else lo - 2
        j = 0 if dx < 0 else 1
        span = pl.ds(2 + CHUNK * piece_r, CHUNK)
        return pltpu.make_async_remote_copy(
            src_ref=buf.at[par, :, span, mine : mine + 2, :],
            dst_ref=buf.at[par, :, span, theirs : theirs + 2, :],
            send_sem=x_send.at[par, j, piece_r], recv_sem=x_recv.at[par, j, piece_r],
            device_id=target(dx, 0), device_id_type=MESH,
        )

    def edge(j, par):
        dx, dy = DIRECTIONS[j]
        side = 1 if dy < 0 else 0
        if dx == 0:
            src = ps.at[par]
            dst = pr.at[par, side, :, lo:hi, :]
        else:
            mine = 0 if dx < 0 else rows - 2
            theirs = hi if dx < 0 else lo - 2
            src = ps.at[par, :, mine : mine + 2, :]
            dst = pr.at[par, side, :, theirs : theirs + 2, :]
        return pltpu.make_async_remote_copy(
            src_ref=src, dst_ref=dst, send_sem=y_send.at[par, j], recv_sem=y_recv.at[par, j],
            device_id=target(dx, dy), device_id_type=MESH,
        )

    def send_face(par, piece_r):
        for dx in (-1, 1):
            @pl.when(exists(dx, 0))
            def _():
                face(dx, par, piece_r).start()

    lane2 = lax.broadcasted_iota(jnp.int32, (rows, cy), 1)
    lanem = lax.rem(lane2, half)

    def send_edges(par):
        for c in range(3):
            packed = jnp.zeros((rows, cy), f32)
            for r in range(nr):
                turned = pltpu.roll(buf[par, c, r + 2, lo:hi, :], 2 + 4 * r, 1)
                packed = jnp.where((lanem >= 4 * r) & (lanem < 4 * r + 4), turned, packed)
            ps[par, c] = packed
        for j in range(2, 8):
            @pl.when(exists(*DIRECTIONS[j]))
            def _():
                edge(j, par).start()

    def wait_halos(par):
        for j, dx in enumerate((-1, 1)):
            @pl.when(exists(dx, 0))
            def _():
                for piece_r in range(chunks):
                    face(dx, par, piece_r).wait_send()
            @pl.when(exists(-dx, 0))
            def _():
                for piece_r in range(chunks):
                    face(dx, par, piece_r).wait_recv()
        for j in range(2, 8):
            dx, dy = DIRECTIONS[j]
            @pl.when(exists(dx, dy))
            def _():
                edge(j, par).wait_send()
            @pl.when(exists(-dx, -dy))
            def _():
                edge(j, par).wait_recv()

    left2 = lane2 < half
    sign = jnp.where(left2, 1.0, -1.0)
    sign1 = jnp.where(left, 1.0, -1.0)
    lm3 = lanem[None]
    lm1 = lax.rem(lane, half)[None]

    def depth_first(plus1, minus1, plus2, minus2, sgn):
        return (B1 * sgn) * (plus1 - minus1) + (B2 * sgn) * (plus2 - minus2)

    def along_y(core, halo, lm):
        return (
            pltpu.roll(jnp.where(lm < 1, halo, core), cy - 1, 2),
            pltpu.roll(jnp.where(lm >= half - 1, halo, core), 1, 2),
            pltpu.roll(jnp.where(lm < 2, halo, core), cy - 2, 2),
            pltpu.roll(jnp.where(lm >= half - 2, halo, core), 2, 2),
        )

    def ghosts(ref, index, span):
        mask = lax.broadcasted_iota(jnp.int32, (span.stop - span.start, cy), 1) < half
        at = lambda r: index + (r + 2, span, slice(None))
        ref[at(-1)] = jnp.where(mask, ref[at(1)], 0.0)
        ref[at(-2)] = jnp.where(mask, ref[at(2)], 0.0)
        ref[at(nr)] = pltpu.roll(ref[at(nr - 1)], half, 1)
        ref[at(nr + 1)] = pltpu.roll(ref[at(nr - 2)], half, 1)

    def grid_step(n, par):
        new = 1 - par
        wait_halos(par)

        ghosts(buf, (par, 0), slice(lo, hi))
        ghosts(buf, (par, 1), slice(lo, hi))
        ghosts(buf, (par, 2), slice(0, hi + cx))

        from_left = lax.rem(lane2, 4) < 2

        def joined(c, at, size):
            take = from_left if size == rows else from_left[0:size]
            return jnp.where(take, pr[par, 0, c, at : at + size, :], pr[par, 1, c, at : at + size, :])

        g = [joined(c, lo, rows) for c in range(3)]
        gx[lo:hi, :] = g[0]
        gx[0:lo, :] = joined(0, 0, cx)
        gx[hi : hi + cx, :] = joined(0, hi, cx)
        g_y = jnp.where(row < 4, joined(1, hi, cx), joined(1, 0, cx))
        a_g = first(
            gx[lo + 1 : hi + 1, :], gx[lo - 1 : hi - 1, :],
            gx[lo + 2 : hi + 2, :], gx[lo - 2 : hi - 2, :],
        )
        spot = lax.div(lanem, 4)
        turn = lambda v, by: pltpu.roll(v, by % cy, 1)
        h0_here = (~left2 & from_left) | (left2 & ~from_left)
        g2 = g[2]
        plus1 = jnp.where(spot == nr - 1, turn(g2, half), turn(g2, -4))
        plus2 = jnp.where(
            spot < nr - 2, turn(g2, -8),
            jnp.where(spot == nr - 2, turn(g2, -(half + 4)), turn(g2, -(half - 4))),
        )
        above = jnp.where(h0_here, turn(g2, -4), 0.0)
        minus1 = jnp.where(spot == 0, above, turn(g2, 4))
        minus2 = jnp.where(
            spot == 0, jnp.where(h0_here, turn(g2, -8), 0.0),
            jnp.where(spot == 1, jnp.where(h0_here, g2, 0.0), turn(g2, 8)),
        )
        t_g = a_g + depth_first(plus1, minus1, plus2, minus2, jnp.where(h0_here, 1.0, -1.0))
        for r in range(nr):
            back = (half - 2 - 4 * r) % cy
            for c in range(3):
                ht[c, r] = turn(g[c], back)
            th[r] = turn(t_g, back)
            hx[r] = turn(g_y, back)

        def u(c, r, shift, at, size=rows):
            return buf[par, c, pl.ds(r + 2 + shift, PLANES), at : at + size, :]

        def prepare(b, carry):
            r = b * PLANES
            x = first(u(0, r, 0, lo + 1), u(0, r, 0, lo - 1), u(0, r, 0, lo + 2), u(0, r, 0, lo - 2))
            y = first(*along_y(u(1, r, 0, lo), ht[1, pl.ds(r, PLANES)], lm3))
            z = depth_first(u(2, r, 1, lo), u(2, r, -1, lo), u(2, r, 2, lo), u(2, r, -2, lo), sign)
            e_ref[pl.ds(r + 2, PLANES)] = x + y
            s_ref[pl.ds(r, PLANES), lo:hi, :] = y + z
            q_ref[pl.ds(r, PLANES)] = x + z

            def mixed(comp, shift):
                return jnp.where(row[None] < 4, u(comp, r, shift, hi, cx), u(comp, r, shift, 0, cx))

            s_halo = first(*along_y(mixed(1, 0), hx[pl.ds(r, PLANES)], lm1)) + depth_first(
                mixed(2, 1), mixed(2, -1), mixed(2, 2), mixed(2, -2), sign1
            )
            s_ref[pl.ds(r, PLANES), 0:lo, :] = s_halo
            s_ref[pl.ds(r, PLANES), hi : hi + cx, :] = s_halo
            return carry

        lax.fori_loop(0, nr // PLANES, prepare, 0)
        ghosts(e_ref, (), slice(0, rows))

        def advance(b, carry):
            r = b * PLANES
            sh = sh_ref[pl.ds(r, PLANES)]
            bk = bk_ref[pl.ds(r, PLANES)]

            def s(at):
                return s_ref[pl.ds(r, PLANES), at : at + rows, :]

            def e(shift):
                return e_ref[pl.ds(r + 2 + shift, PLANES)]

            for c in range(3):
                mid = u(c, r, 0, lo)
                y = along_y(mid, ht[c, pl.ds(r, PLANES)], lm3)
                near = [u(c, r, 0, lo + 1) + u(c, r, 0, lo - 1), y[0] + y[1], u(c, r, 1, lo) + u(c, r, -1, lo)]
                far = [u(c, r, 0, lo + 2) + u(c, r, 0, lo - 2), y[2] + y[3], u(c, r, 2, lo) + u(c, r, -2, lo)]
                lap = (3.0 * A0) * mid + A1 * (near[0] + near[1] + near[2]) + A2 * (far[0] + far[1] + far[2])
                own_second = A0 * mid + A1 * near[c] + A2 * far[c]
                if c == 0:
                    cross = first(s(lo + 1), s(lo - 1), s(lo + 2), s(lo - 2))
                elif c == 1:
                    cross = first(*along_y(q_ref[pl.ds(r, PLANES)], th[pl.ds(r, PLANES)], lm3))
                else:
                    cross = depth_first(e(1), e(-1), e(2), e(-2), sign)
                acc = sh * lap + bk * (own_second + cross)
                place = (new, c, pl.ds(r + 2, PLANES), slice(lo, hi), slice(None))
                buf[place] = 2.0 * mid - buf[place] + acc
            return carry

        for piece_r in range(chunks):
            lax.fori_loop(piece_r * CHUNK // PLANES, (piece_r + 1) * CHUNK // PLANES, advance, 0)

            @pl.when(n < steps - 1)
            def _():
                send_face(new, piece_r)

        @pl.when(n < steps - 1)
        def _():
            send_edges(new)

    def surface_copy(moment, par, da, dg):
        to_a, to_g = lax.rem(a + da, 2), lax.rem(gy + dg, gys)
        at = pl.ds(pl.multiple_of(lo + cx * to_a, cx), cx)
        return pltpu.make_async_remote_copy(
            src_ref=buf.at[par, :, 2, at, :], dst_ref=surf.at[moment, piece],
            send_sem=surf_send.at[moment, gys * da + dg], recv_sem=surf_recv.at[moment, gys * da + dg],
            device_id=(2 * k + to_a, to_g), device_id_type=MESH,
        )

    def send_surface(moment, par):
        for da, dg, _ in row_mates():
            surface_copy(moment, par, da, dg).start()
        surf[moment, piece] = buf[par, :, 2, own_buf, :]

    def gather_motion(moment, par):
        for da, dg, _ in row_mates():
            surface_copy(moment, par, da, dg).wait()
        for j in range(gys):
            for c in range(3):
                even, odd = surf[moment, 2 * j, c], surf[moment, 2 * j + 1, c]
                table = jnp.where(left, even, pltpu.roll(odd, half, 1))
                for part in range(3):
                    piece_of = table.astype(bf16)
                    at = 24 * part + 8 * c
                    lhs[at : at + 8, 128 * j : 128 * (j + 1)] = piece_of.astype(f32)
                    table = table - piece_of.astype(f32)
        found = jnp.dot(lhs[...].astype(bf16), hot[...], preferred_element_type=f32)
        for c in range(3):
            value = found[8 * c : 8 * c + 8] + found[24 + 8 * c : 32 + 8 * c]
            value = value + found[48 + 8 * c : 56 + 8 * c]
            value = jnp.sum(value * hotx[...], axis=0, keepdims=True) * SCALE
            mot[moment, 2 * c : 2 * c + 1, :] = value
            mot[moment, 2 * c + 1 : 2 * c + 2, :] = value

    def unit_span(unit):
        return pl.ds(pl.multiple_of(lax.div(unit, COUPLINGS) * UNIT, UNIT), UNIT), COUPLINGS - 1 - lax.rem(unit, COUPLINGS)

    def g_copy(ref, device, send_sem, recv_sem):
        return pltpu.make_async_remote_copy(
            src_ref=ref, dst_ref=ref, send_sem=send_sem, recv_sem=recv_sem,
            device_id=device, device_id_type=MESH,
        )

    def spread(unit, dk):
        span, moment = unit_span(unit)
        ref = g_all.at[k, a, yb, cb, span, moment, 0:g_rows, :]
        return g_copy(
            ref, (2 * lax.rem(k + dk, pairs) + a, gy), near_send.at[unit, dk - 1], near_recv.at[unit, dk - 1]
        )

    y_mate = (slab, 2 * (1 - yb) + cb)
    c_mate = (slab, 2 * yb + 1 - cb)

    def hop(unit, phase, even):
        span, moment = unit_span(unit)
        tail = (span, moment, slice(0, g_rows), slice(None))
        if phase == 0:
            ref, device = g_all.at[(slice(None), a, yb, cb) + tail], mate if even else y_mate
        elif phase == 1 and even:
            ref, device = g_all.at[(slice(None), slice(None), yb, cb) + tail], y_mate
        elif phase == 1:
            ref, device = g_all.at[(slice(None), a, slice(None), cb) + tail], mate
        else:
            ref, device = g_all.at[(slice(None), slice(None), slice(None), cb) + tail], c_mate
        return g_copy(ref, device, hop_send.at[unit, phase], hop_recv.at[unit, phase])

    def respond(unit):
        stage = lax.rem(unit, COUPLINGS)
        group = lax.div(unit, COUPLINGS)

        @pl.when(stage == 0)
        def _():
            for i in range(UNIT):
                vs[i, 0:3, :] = force[group * UNIT + i] * (1.0 / SCALE)

        v = [vs[i] for i in range(UNIT)]
        total = list(v)
        for it in range(SUB):
            for i in range(UNIT):
                high = v[i].astype(bf16)
                low = (v[i] - high.astype(f32)).astype(bf16)
                both = jnp.concatenate([high, low], axis=0)
                got = lax.dot_general(
                    both, t_ref[group * UNIT + i], (((1,), (1,)), ((), ())), preferred_element_type=f32
                )
                v[i] = got[0:8] + got[8:16]
                if it < SUB - 1:
                    total[i] = total[i] + v[i]
        for i in range(UNIT):
            result = jnp.where(stage == 0, total[i], v[i])
            vs[i] = result
            for c in range(3):
                for h in range(2):
                    g_all[k, a, yb, cb, group * UNIT + i, COUPLINGS - 1 - stage, 2 * c + h : 2 * c + h + 1, :] = (
                        result[c : c + 1, 128 * h : 128 * (h + 1)]
                    )

    def tick(i):
        @pl.when(i < units)
        def _():
            respond(i)
            for dk in range(1, pairs):
                spread(i, dk).start()

        for phase in range(4):
            unit = i - 1 - phase
            for even in (True, False):
                @pl.when((unit >= 0) & (unit < units) & (lax.rem(unit + units, 2) == (0 if even else 1)))
                def _():
                    if phase == 0:
                        for dk in range(1, pairs):
                            spread(unit, dk).wait_recv()
                    else:
                        hop(unit, phase - 1, even).wait_recv()
                    if phase < 3:
                        hop(unit, phase, even).start()

    def body(i, carry):
        n = i - EARLY
        par = lax.rem(n + 2 * EARLY, 2)

        @pl.when(n == 0)
        def _():
            for j in range(8):
                give(j).wait()
            for piece_r in range(chunks):
                send_face(0, piece_r)
            send_edges(0)

        @pl.when(n >= 0)
        def _():
            grid_step(n, par)

        @pl.when((n >= 0) & (lax.rem(n + EARLY * EVERY, EVERY) == EVERY - 1))
        def _():
            send_surface(lax.div(n, EVERY), 1 - par)

        tick(i)

        @pl.when((n > 0) & (lax.rem(n + EARLY * EVERY, EVERY) == EVERY - 1) & (n < steps - 1))
        def _():
            gather_motion(lax.div(n, EVERY), 1 - par)
        return carry

    lax.fori_loop(0, EARLY + steps, body, 0)

    last = steps % 2
    theirs = pl.ds(pl.multiple_of(lo + cx * (1 - a), cx), cx)
    back = pltpu.make_async_remote_copy(
        src_ref=buf.at[last, :, 2 : nr + 2, theirs, :], dst_ref=fold,
        send_sem=back_send.at[0], recv_sem=back_recv.at[0], device_id=mate, device_id_type=MESH,
    )
    back.start()
    gather_motion(COUPLINGS - 1, last)

    for unit in range(units):
        for dk in range(1, pairs):
            spread(unit, dk).wait_send()
        for phase in range(3):
            hop(unit, phase, unit % 2 == 0).wait_send()

    table = g_all.reshape(slabs * gys * arch, COUPLINGS, 8, 128)
    row8 = lax.broadcasted_iota(jnp.int32, (8, 128), 0)

    def tile(j, carry):
        lanes = pl.ds(pl.multiple_of(128 * j, 128), 128)
        motion = [mot[m, :, lanes] for m in range(COUPLINGS)]

        def eight(i, motion):
            base = pl.multiple_of(128 * j + 8 * i, 8)
            out = [jnp.zeros((8, 128), f32)] * 2
            for b in range(8):
                kind = kind_ref[base + b]
                got = None
                for m in range(COUPLINGS):
                    term = jnp.broadcast_to(motion[m][:, b : b + 1], (8, 128)) * table[kind, m]
                    got = term if got is None else got + term
                got = jnp.where(row8 < g_rows, got, 0.0)
                got = got + pltpu.roll(got, 4, 0)
                got = got + pltpu.roll(got, 2, 0)
                moved = pltpu.roll(got, 1, 0)
                here, there = (got, moved) if b % 2 == 0 else (moved, got)
                out = [jnp.where(row8 == b, one, so_far) for one, so_far in zip((here, there), out)]
            o_ref[pl.ds(base, 8), 0:128] = out[0]
            o_ref[pl.ds(base, 8), 128:256] = out[1]
            return tuple(pltpu.roll(one, 120, 1) for one in motion)

        lax.fori_loop(0, 16, eight, tuple(motion))
        return carry

    lax.fori_loop(0, count // 128, tile, 0)

    back.wait()
    for c in range(3):
        for r in range(nr):
            mine, other = buf[last, c, r + 2, own_buf, :], fold[c, r]
            lower = jnp.where(hsel == 0, mine, other)
            upper = jnp.where(hsel == 0, other, mine)
            f_ref[c, r] = jnp.where(left, lower, pltpu.roll(upper, half, 1))
            f_ref[c, nz - 1 - r] = jnp.where(left, pltpu.roll(lower, half, 1), upper)


def per_device(
    displacement, previous, shear_coef, bulk_coef, cell_index, archetype_id, transition, forcing
):
    _, nz, cx, cy = displacement.shape
    arch, width, _ = transition.shape
    count = cell_index.shape[0]
    slabs, gys = lax.axis_size("slab"), lax.axis_size("gy")
    pairs, nr, rows = slabs // 2, nz // 2, 2 * cx
    tall = rows + 2 * cx
    units = arch // UNIT * COUPLINGS
    chunks = nr // CHUNK
    f32 = jnp.float32
    vmem, dma = pltpu.VMEM, pltpu.SemaphoreType.DMA
    whole = pl.BlockSpec(memory_space=pltpu.VMEM)
    away = pl.BlockSpec(memory_space=pl.ANY)
    return pl.pallas_call(
        city_kernel,
        out_shape=(
            jax.ShapeDtypeStruct(displacement.shape, f32),
            jax.ShapeDtypeStruct((count, width), f32),
        ),
        in_specs=[away] * 4 + [whole, pl.BlockSpec(memory_space=pltpu.SMEM), away, away],
        out_specs=(whole, whole),
        scratch_shapes=[
            vmem((8, nz, cx, cy), f32),
            vmem((arch, width, width), jnp.bfloat16),
            vmem((arch, 3, width), f32),
            vmem((8, nr, cx, cy), f32),
            vmem((2, 3, nr + 4, tall, cy), f32),
            vmem((nr, rows, cy), f32),
            vmem((nr, rows, cy), f32),
            vmem((2, 3, rows, cy), f32),
            vmem((2, 2, 3, tall, cy), f32),
            vmem((tall, cy), f32),
            vmem((3, nr, rows, cy), f32),
            vmem((nr, rows, cy), f32),
            vmem((nr, cx, cy), f32),
            vmem((nr + 4, rows, cy), f32),
            vmem((nr, tall, cy), f32),
            vmem((nr, rows, cy), f32),
            vmem((UNIT, 8, width), f32),
            vmem((pairs, 2, 2, gys // 2, arch, COUPLINGS, 8, 128), f32),
            vmem((COUPLINGS, 2 * gys, 3, cx, cy), f32),
            vmem((gys * cy, count), jnp.bfloat16),
            vmem((cx, count), f32),
            vmem((72, gys * cy), f32),
            vmem((COUPLINGS, 8, count), f32),
            vmem((3, nr, cx, cy), f32),
            dma((6,)),
            dma((8,)),
            dma((8,)),
            dma((2, 2, chunks)),
            dma((2, 2, chunks)),
            dma((2, 8)),
            dma((2, 8)),
            dma((units, pairs - 1)),
            dma((units, pairs - 1)),
            dma((units, 3)),
            dma((units, 3)),
            dma((COUPLINGS, 2 * gys)),
            dma((COUPLINGS, 2 * gys)),
            dma((1,)),
            dma((1,)),
        ],
        compiler_params=pltpu.CompilerParams(
            collective_id=0, has_side_effects=True, vmem_limit_bytes=60 * 1024 * 1024
        ),
    )(
        displacement, previous, shear_coef, bulk_coef, cell_index.reshape(1, count),
        archetype_id[:, 0], transition, forcing,
    )


def solution(mesh):
    in_specs = (
        P(None, None, "slab", "gy"),
        P(None, None, "slab", "gy"),
        P(None, "slab", "gy"),
        P(None, "slab", "gy"),
        P(("slab", "gy")),
        P(("slab", "gy"), None),
        P(("slab", "gy"), None, None),
        P(("slab", "gy"), None, None),
    )
    out_specs = (P(None, None, "slab", "gy"), P(("slab", "gy"), None))
    return jax.shard_map(
        per_device, mesh=mesh, in_specs=in_specs, out_specs=out_specs, check_vma=False
    )
```

time: 309 us -> 251 us (0.81)
  waiting for transfers between devices: 41.6 us -> 0 us
  Pallas kernels: 220 us -> 244 us
  local copies, waits for them, and re-layouts: 21.5 us -> 5.65 us
  starting transfers between devices: 12.9 us -> 0 us
  blocking collectives: 5.6 us -> 0 us
  other arithmetic: 5.23 us -> 0 us
    all_to_all x3 -> x0, waiting for transfers between devices: 41.6 us -> none  [the longest x2 35.4 us: per_device(): lax.all_to_all(states, ('slab', 'gy'), split_axis=0, concat_axis=0, tiled...]
    pallas_call x3 -> x1, Pallas kernels: 220 us -> 244 us  [per_device(): pl.pallas_call(city_kernel, out_shape=(jax.ShapeDtypeStruct(displacement....]
    all_to_all x3 -> x0, starting transfers between devices: 12.9 us -> none  [the longest x1 6.73 us: per_device(): lax.all_to_all(motion, ('slab', 'gy'), split_axis=0, concat_axis=0, tiled...]
    gather x2 -> x0, local copies, waits for them, and re-layouts: 10.1 us -> none  [the longest x1 5.47 us: per_device(): motion = jnp.take(table, slot_cell, axis=0, mode='clip')]
    all_gather x1 -> x0, blocking collectives: 5.6 us -> none  [per_device(): surface = lax.all_gather(surface, 'gy', axis=3, tiled=True)]
    unnamed x18 -> x3, local copies, waits for them, and re-layouts: 8.21 us -> 5.65 us
  transfers between devices with their start and end apart: 3 -> 0, of which waited for: 3 -> 0; matrix products, arithmetic and copies ran while one was open for 1% -> 0% of each run, Pallas kernels for 5% -> 0%
where the time goes in v1:
time: 251 us
  Pallas kernels  244 us (97%)
  local copies, waits for them, and re-layouts  5.65 us (2%)
    pallas_call x1, Pallas kernels, per_device(): pl.pallas_call(city_kernel, out_shape=(jax.ShapeDtypeStruct(displacement....  244 us
    unnamed x3, local copies, waits for them, and re-layouts  5.65 us

profile of v1, /device:TPU:0, one launch (start us, length us, event | category | flops | bytes accessed | tf_op | source)
XLA Modules:
  0.0 250.5 jit_solution(6348322109476715439)
XLA Ops:
  0.6 1.6 copy.10.f_hbm
  2.2 244.2 %shard_map.95 = (f32[3,32,8,128]{3,2,1,0:T(8,128)}, f32[1024,256]{1,0:T(8,128)}) custom-call(f32[3,32,8,128]{3,2,1,0:T(8,128)} %d_hbm.1, f32[3,32,8,128]{3,2,1,0:T(8,128)} %p_hbm.1, f32[32,8,128]{2,1,0:T(8,128)} %sh_hbm.1, f32[32,8,128]{2,1,0:T(8,128)} %bk_hbm.1, s32[1,1024]{1,0:T(1,128)} %bitcast.2, s32[1024]{0:T(1024)} %bitcast.3, ...), custom_call_target="tpu_custom_call" | custom-call | tf_op jit(solution)/shard_map/pallas_call | solution.py:599
  246.5 1.8 copy.13
  248.3 2.3 copy.14

commit v2 on v1

--- a/solution.py
+++ b/solution.py
@@ -13,8 +13,10 @@
 UNIT = 8
 EARLY = 5
 CHUNK = 4
-PLANES = 1
+PREPARE = 16
+ADVANCE = 4
 SCALE = 2.0 ** 60
+LEGS = ((0, 1), (2, 3), (4,))
 
 A0, A1, A2 = -30.0 / 12.0, 16.0 / 12.0, -1.0 / 12.0
 B1, B2 = 8.0 / 12.0, -1.0 / 12.0
@@ -314,45 +316,49 @@
             th[r] = turn(t_g, back)
             hx[r] = turn(g_y, back)
 
-        def u(c, r, shift, at, size=rows):
-            return buf[par, c, pl.ds(r + 2 + shift, PLANES), at : at + size, :]
+        def reader(planes):
+            def u(c, r, shift, at, size=rows):
+                return buf[par, c, pl.ds(r + 2 + shift, planes), at : at + size, :]
+            return u
 
         def prepare(b, carry):
-            r = b * PLANES
+            u, planes = reader(PREPARE), PREPARE
+            r = b * PREPARE
             x = first(u(0, r, 0, lo + 1), u(0, r, 0, lo - 1), u(0, r, 0, lo + 2), u(0, r, 0, lo - 2))
-            y = first(*along_y(u(1, r, 0, lo), ht[1, pl.ds(r, PLANES)], lm3))
+            y = first(*along_y(u(1, r, 0, lo), ht[1, pl.ds(r, planes)], lm3))
             z = depth_first(u(2, r, 1, lo), u(2, r, -1, lo), u(2, r, 2, lo), u(2, r, -2, lo), sign)
-            e_ref[pl.ds(r + 2, PLANES)] = x + y
-            s_ref[pl.ds(r, PLANES), lo:hi, :] = y + z
-            q_ref[pl.ds(r, PLANES)] = x + z
+            e_ref[pl.ds(r + 2, planes)] = x + y
+            s_ref[pl.ds(r, planes), lo:hi, :] = y + z
+            q_ref[pl.ds(r, planes)] = x + z
 
             def mixed(comp, shift):
                 return jnp.where(row[None] < 4, u(comp, r, shift, hi, cx), u(comp, r, shift, 0, cx))
 
-            s_halo = first(*along_y(mixed(1, 0), hx[pl.ds(r, PLANES)], lm1)) + depth_first(
+            s_halo = first(*along_y(mixed(1, 0), hx[pl.ds(r, planes)], lm1)) + depth_first(
                 mixed(2, 1), mixed(2, -1), mixed(2, 2), mixed(2, -2), sign1
             )
-            s_ref[pl.ds(r, PLANES), 0:lo, :] = s_halo
-            s_ref[pl.ds(r, PLANES), hi : hi + cx, :] = s_halo
+            s_ref[pl.ds(r, planes), 0:lo, :] = s_halo
+            s_ref[pl.ds(r, planes), hi : hi + cx, :] = s_halo
             return carry
 
-        lax.fori_loop(0, nr // PLANES, prepare, 0)
+        lax.fori_loop(0, nr // PREPARE, prepare, 0)
         ghosts(e_ref, (), slice(0, rows))
 
         def advance(b, carry):
-            r = b * PLANES
-            sh = sh_ref[pl.ds(r, PLANES)]
-            bk = bk_ref[pl.ds(r, PLANES)]
+            u, planes = reader(ADVANCE), ADVANCE
+            r = b * ADVANCE
+            sh = sh_ref[pl.ds(r, planes)]
+            bk = bk_ref[pl.ds(r, planes)]
 
             def s(at):
-                return s_ref[pl.ds(r, PLANES), at : at + rows, :]
+                return s_ref[pl.ds(r, planes), at : at + rows, :]
 
             def e(shift):
-                return e_ref[pl.ds(r + 2 + shift, PLANES)]
+                return e_ref[pl.ds(r + 2 + shift, planes)]
 
             for c in range(3):
                 mid = u(c, r, 0, lo)
-                y = along_y(mid, ht[c, pl.ds(r, PLANES)], lm3)
+                y = along_y(mid, ht[c, pl.ds(r, planes)], lm3)
                 near = [u(c, r, 0, lo + 1) + u(c, r, 0, lo - 1), y[0] + y[1], u(c, r, 1, lo) + u(c, r, -1, lo)]
                 far = [u(c, r, 0, lo + 2) + u(c, r, 0, lo - 2), y[2] + y[3], u(c, r, 2, lo) + u(c, r, -2, lo)]
                 lap = (3.0 * A0) * mid + A1 * (near[0] + near[1] + near[2]) + A2 * (far[0] + far[1] + far[2])
@@ -360,16 +366,16 @@
                 if c == 0:
                     cross = first(s(lo + 1), s(lo - 1), s(lo + 2), s(lo - 2))
                 elif c == 1:
-                    cross = first(*along_y(q_ref[pl.ds(r, PLANES)], th[pl.ds(r, PLANES)], lm3))
+                    cross = first(*along_y(q_ref[pl.ds(r, planes)], th[pl.ds(r, planes)], lm3))
                 else:
                     cross = depth_first(e(1), e(-1), e(2), e(-2), sign)
                 acc = sh * lap + bk * (own_second + cross)
-                place = (new, c, pl.ds(r + 2, PLANES), slice(lo, hi), slice(None))
+                place = (new, c, pl.ds(r + 2, planes), slice(lo, hi), slice(None))
                 buf[place] = 2.0 * mid - buf[place] + acc
             return carry
 
         for piece_r in range(chunks):
-            lax.fori_loop(piece_r * CHUNK // PLANES, (piece_r + 1) * CHUNK // PLANES, advance, 0)
+            lax.fori_loop(piece_r * CHUNK // ADVANCE, (piece_r + 1) * CHUNK // ADVANCE, advance, 0)
 
             @pl.when(n < steps - 1)
             def _():
@@ -432,18 +438,21 @@
     y_mate = (slab, 2 * (1 - yb) + cb)
     c_mate = (slab, 2 * yb + 1 - cb)
 
-    def hop(unit, phase, even):
+    def hop(unit, leg):
         span, moment = unit_span(unit)
+        phase, even = divmod(leg, 2)
+        if phase < 2:
+            span = pl.ds(span.start + (0 if even == 0 else UNIT // 2), UNIT // 2)
         tail = (span, moment, slice(0, g_rows), slice(None))
+        every = slice(None)
         if phase == 0:
-            ref, device = g_all.at[(slice(None), a, yb, cb) + tail], mate if even else y_mate
-        elif phase == 1 and even:
-            ref, device = g_all.at[(slice(None), slice(None), yb, cb) + tail], y_mate
+            ref, device = g_all.at[(every, a, yb, cb) + tail], (mate, y_mate)[even]
         elif phase == 1:
-            ref, device = g_all.at[(slice(None), a, slice(None), cb) + tail], mate
+            ref = g_all.at[((every, every, yb, cb) if even == 0 else (every, a, every, cb)) + tail]
+            device = (y_mate, mate)[even]
         else:
-            ref, device = g_all.at[(slice(None), slice(None), slice(None), cb) + tail], c_mate
-        return g_copy(ref, device, hop_send.at[unit, phase], hop_recv.at[unit, phase])
+            ref, device = g_all.at[(every, every, every, cb) + tail], c_mate
+        return g_copy(ref, device, hop_send.at[unit, leg], hop_recv.at[unit, leg])
 
     def respond(unit):
         stage = lax.rem(unit, COUPLINGS)
@@ -485,16 +494,18 @@
 
         for phase in range(4):
             unit = i - 1 - phase
-            for even in (True, False):
-                @pl.when((unit >= 0) & (unit < units) & (lax.rem(unit + units, 2) == (0 if even else 1)))
-                def _():
-                    if phase == 0:
-                        for dk in range(1, pairs):
-                            spread(unit, dk).wait_recv()
-                    else:
-                        hop(unit, phase - 1, even).wait_recv()
-                    if phase < 3:
-                        hop(unit, phase, even).start()
+
+            @pl.when((unit >= 0) & (unit < units))
+            def _():
+                if phase == 0:
+                    for dk in range(1, pairs):
+                        spread(unit, dk).wait_recv()
+                else:
+                    for leg in LEGS[phase - 1]:
+                        hop(unit, leg).wait_recv()
+                if phase < 3:
+                    for leg in LEGS[phase]:
+                        hop(unit, leg).start()
 
     def body(i, carry):
         n = i - EARLY
@@ -537,8 +548,8 @@
     for unit in range(units):
         for dk in range(1, pairs):
             spread(unit, dk).wait_send()
-        for phase in range(3):
-            hop(unit, phase, unit % 2 == 0).wait_send()
+        for leg in range(5):
+            hop(unit, leg).wait_send()
 
     table = g_all.reshape(slabs * gys * arch, COUPLINGS, 8, 128)
     row8 = lax.broadcasted_iota(jnp.int32, (8, 128), 0)
@@ -547,14 +558,15 @@
         lanes = pl.ds(pl.multiple_of(128 * j, 128), 128)
         motion = [mot[m, :, lanes] for m in range(COUPLINGS)]
 
-        def eight(i, motion):
+        for i in range(16):
             base = pl.multiple_of(128 * j + 8 * i, 8)
             out = [jnp.zeros((8, 128), f32)] * 2
             for b in range(8):
-                kind = kind_ref[base + b]
+                kind = kind_ref[128 * j + 8 * i + b]
                 got = None
                 for m in range(COUPLINGS):
-                    term = jnp.broadcast_to(motion[m][:, b : b + 1], (8, 128)) * table[kind, m]
+                    at = 8 * i + b
+                    term = jnp.broadcast_to(motion[m][:, at : at + 1], (8, 128)) * table[kind, m]
                     got = term if got is None else got + term
                 got = jnp.where(row8 < g_rows, got, 0.0)
                 got = got + pltpu.roll(got, 4, 0)
@@ -564,9 +576,6 @@
                 out = [jnp.where(row8 == b, one, so_far) for one, so_far in zip((here, there), out)]
             o_ref[pl.ds(base, 8), 0:128] = out[0]
             o_ref[pl.ds(base, 8), 128:256] = out[1]
-            return tuple(pltpu.roll(one, 120, 1) for one in motion)
-
-        lax.fori_loop(0, 16, eight, tuple(motion))
         return carry
 
     lax.fori_loop(0, count // 128, tile, 0)
@@ -638,8 +647,8 @@
             dma((2, 8)),
             dma((units, pairs - 1)),
             dma((units, pairs - 1)),
-            dma((units, 3)),
-            dma((units, 3)),
+            dma((units, 5)),
+            dma((units, 5)),
             dma((COUPLINGS, 2 * gys)),
             dma((COUPLINGS, 2 * gys)),
             dma((1,)),

time: 251 us -> 153 us (0.61)
  Pallas kernels: 244 us -> 147 us
    pallas_call x1, Pallas kernels: 244 us -> 147 us  [per_device(): pl.pallas_call(city_kernel, out_shape=(jax.ShapeDtypeStruct(displacement....]
where the time goes in v2:
time: 153 us
  Pallas kernels  147 us (96%)
  local copies, waits for them, and re-layouts  5.65 us (4%)
    pallas_call x1, Pallas kernels, per_device(): pl.pallas_call(city_kernel, out_shape=(jax.ShapeDtypeStruct(displacement....  147 us
    unnamed x3, local copies, waits for them, and re-layouts  5.65 us

profile of v2, /device:TPU:0, one launch (start us, length us, event | category | flops | bytes accessed | tf_op | source)
XLA Modules:
  0.0 153.1 jit_solution(16869782386849655544)
XLA Ops:
  0.6 1.6 %copy.10.f_hbm = f32[32,3,256]{2,1,0:T(4,128)} copy(f32[32,3,256]{2,0,1:T(8,128)} %param.15) | data formatting | bytes 196608 | tf_op args[7]
  2.2 146.9 %shard_map.95 = (f32[3,32,8,128]{3,2,1,0:T(8,128)}, f32[1024,256]{1,0:T(8,128)}) custom-call(f32[3,32,8,128]{3,2,1,0:T(8,128)} %d_hbm.1, f32[3,32,8,128]{3,2,1,0:T(8,128)} %p_hbm.1, f32[32,8,128]{2,1,0:T(8,128)} %sh_hbm.1, f32[32,8,128]{2,1,0:T(8,128)} %bk_hbm.1, s32[1,1024]{1,0:T(1,128)} %bitcast.2, s32[1024]{0:T(1024)} %bitcast.3, ...), custom_call_target="tpu_custom_call" | custom-call | tf_op jit(solution)/shard_map/pallas_call | solution.py:608
  149.1 1.8 %copy.13 = f32[3,32,8,128]{3,2,1,0:T(8,128)} copy(f32[3,32,8,128]{3,2,1,0:T(8,128)} %get-tuple-element.4) | data formatting | bytes 786432
  150.9 2.3 %copy.14 = f32[1024,256]{1,0:T(8,128)} copy(f32[1024,256]{1,0:T(8,128)} %get-tuple-element.5) | data formatting | bytes 2097152

commit v3 on v2

--- a/solution.py
+++ b/solution.py
@@ -12,8 +12,8 @@
 SUB = 6
 UNIT = 8
 EARLY = 5
-CHUNK = 4
-PREPARE = 16
+CHUNK = 8
+FACE = 4
 ADVANCE = 4
 SCALE = 2.0 ** 60
 LEGS = ((0, 1), (2, 3), (4,))
@@ -181,7 +181,7 @@
         mine = lo if dx < 0 else hi - 2
         theirs = hi if dx < 0 else lo - 2
         j = 0 if dx < 0 else 1
-        span = pl.ds(2 + CHUNK * piece_r, CHUNK)
+        span = pl.ds(2 + FACE * piece_r, FACE)
         return pltpu.make_async_remote_copy(
             src_ref=buf.at[par, :, span, mine : mine + 2, :],
             dst_ref=buf.at[par, :, span, theirs : theirs + 2, :],
@@ -189,19 +189,19 @@
             device_id=target(dx, 0), device_id_type=MESH,
         )
 
-    def edge(j, par):
+    def edge(j, par, piece_r):
         dx, dy = DIRECTIONS[j]
         side = 1 if dy < 0 else 0
         if dx == 0:
-            src = ps.at[par]
-            dst = pr.at[par, side, :, lo:hi, :]
+            src = ps.at[par, piece_r]
+            dst = pr.at[par, piece_r, side, :, lo:hi, :]
         else:
             mine = 0 if dx < 0 else rows - 2
             theirs = hi if dx < 0 else lo - 2
-            src = ps.at[par, :, mine : mine + 2, :]
-            dst = pr.at[par, side, :, theirs : theirs + 2, :]
+            src = ps.at[par, piece_r, :, mine : mine + 2, :]
+            dst = pr.at[par, piece_r, side, :, theirs : theirs + 2, :]
         return pltpu.make_async_remote_copy(
-            src_ref=src, dst_ref=dst, send_sem=y_send.at[par, j], recv_sem=y_recv.at[par, j],
+            src_ref=src, dst_ref=dst, send_sem=y_send.at[par, piece_r, j], recv_sem=y_recv.at[par, piece_r, j],
             device_id=target(dx, dy), device_id_type=MESH,
         )
 
@@ -214,36 +214,37 @@
     lane2 = lax.broadcasted_iota(jnp.int32, (rows, cy), 1)
     lanem = lax.rem(lane2, half)
 
-    def send_edges(par):
+    def send_edges(par, piece_r):
         for c in range(3):
             packed = jnp.zeros((rows, cy), f32)
-            for r in range(nr):
+            for r in range(CHUNK * piece_r, CHUNK * (piece_r + 1)):
                 turned = pltpu.roll(buf[par, c, r + 2, lo:hi, :], 2 + 4 * r, 1)
                 packed = jnp.where((lanem >= 4 * r) & (lanem < 4 * r + 4), turned, packed)
-            ps[par, c] = packed
+            ps[par, piece_r, c] = packed
         for j in range(2, 8):
             @pl.when(exists(*DIRECTIONS[j]))
             def _():
-                edge(j, par).start()
-
-    def wait_halos(par):
+                edge(j, par, piece_r).start()
+
+    def wait_halos(par, piece_r):
         for j, dx in enumerate((-1, 1)):
+            parts = range(piece_r * CHUNK // FACE, (piece_r + 1) * CHUNK // FACE)
             @pl.when(exists(dx, 0))
             def _():
-                for piece_r in range(chunks):
-                    face(dx, par, piece_r).wait_send()
+                for part in parts:
+                    face(dx, par, part).wait_send()
             @pl.when(exists(-dx, 0))
             def _():
-                for piece_r in range(chunks):
-                    face(dx, par, piece_r).wait_recv()
+                for part in parts:
+                    face(dx, par, part).wait_recv()
         for j in range(2, 8):
             dx, dy = DIRECTIONS[j]
             @pl.when(exists(dx, dy))
             def _():
-                edge(j, par).wait_send()
+                edge(j, par, piece_r).wait_send()
             @pl.when(exists(-dx, -dy))
             def _():
-                edge(j, par).wait_recv()
+                edge(j, par, piece_r).wait_recv()
 
     left2 = lane2 < half
     sign = jnp.where(left2, 1.0, -1.0)
@@ -262,68 +263,76 @@
             pltpu.roll(jnp.where(lm >= half - 2, halo, core), 2, 2),
         )
 
-    def ghosts(ref, index, span):
-        mask = lax.broadcasted_iota(jnp.int32, (span.stop - span.start, cy), 1) < half
+    def ghosts(ref, index, span, top):
         at = lambda r: index + (r + 2, span, slice(None))
-        ref[at(-1)] = jnp.where(mask, ref[at(1)], 0.0)
-        ref[at(-2)] = jnp.where(mask, ref[at(2)], 0.0)
-        ref[at(nr)] = pltpu.roll(ref[at(nr - 1)], half, 1)
-        ref[at(nr + 1)] = pltpu.roll(ref[at(nr - 2)], half, 1)
+        if top:
+            mask = lax.broadcasted_iota(jnp.int32, (span.stop - span.start, cy), 1) < half
+            ref[at(-1)] = jnp.where(mask, ref[at(1)], 0.0)
+            ref[at(-2)] = jnp.where(mask, ref[at(2)], 0.0)
+        else:
+            ref[at(nr)] = pltpu.roll(ref[at(nr - 1)], half, 1)
+            ref[at(nr + 1)] = pltpu.roll(ref[at(nr - 2)], half, 1)
+
+    from_left = lax.rem(lane2, 4) < 2
+    spot = lax.div(lanem, 4)
+    turn = lambda v, by: pltpu.roll(v, by % cy, 1)
+    h0_here = (~left2 & from_left) | (left2 & ~from_left)
 
     def grid_step(n, par):
         new = 1 - par
-        wait_halos(par)
-
-        ghosts(buf, (par, 0), slice(lo, hi))
-        ghosts(buf, (par, 1), slice(lo, hi))
-        ghosts(buf, (par, 2), slice(0, hi + cx))
-
-        from_left = lax.rem(lane2, 4) < 2
-
-        def joined(c, at, size):
-            take = from_left if size == rows else from_left[0:size]
-            return jnp.where(take, pr[par, 0, c, at : at + size, :], pr[par, 1, c, at : at + size, :])
-
-        g = [joined(c, lo, rows) for c in range(3)]
-        gx[lo:hi, :] = g[0]
-        gx[0:lo, :] = joined(0, 0, cx)
-        gx[hi : hi + cx, :] = joined(0, hi, cx)
-        g_y = jnp.where(row < 4, joined(1, hi, cx), joined(1, 0, cx))
-        a_g = first(
-            gx[lo + 1 : hi + 1, :], gx[lo - 1 : hi - 1, :],
-            gx[lo + 2 : hi + 2, :], gx[lo - 2 : hi - 2, :],
-        )
-        spot = lax.div(lanem, 4)
-        turn = lambda v, by: pltpu.roll(v, by % cy, 1)
-        h0_here = (~left2 & from_left) | (left2 & ~from_left)
-        g2 = g[2]
-        plus1 = jnp.where(spot == nr - 1, turn(g2, half), turn(g2, -4))
-        plus2 = jnp.where(
-            spot < nr - 2, turn(g2, -8),
-            jnp.where(spot == nr - 2, turn(g2, -(half + 4)), turn(g2, -(half - 4))),
-        )
-        above = jnp.where(h0_here, turn(g2, -4), 0.0)
-        minus1 = jnp.where(spot == 0, above, turn(g2, 4))
-        minus2 = jnp.where(
-            spot == 0, jnp.where(h0_here, turn(g2, -8), 0.0),
-            jnp.where(spot == 1, jnp.where(h0_here, g2, 0.0), turn(g2, 8)),
-        )
-        t_g = a_g + depth_first(plus1, minus1, plus2, minus2, jnp.where(h0_here, 1.0, -1.0))
-        for r in range(nr):
-            back = (half - 2 - 4 * r) % cy
-            for c in range(3):
-                ht[c, r] = turn(g[c], back)
-            th[r] = turn(t_g, back)
-            hx[r] = turn(g_y, back)
+
+        def received(c, at, size, piece_r):
+            return jnp.where(
+                from_left[0:size], pr[par, piece_r, 0, c, at : at + size, :],
+                pr[par, piece_r, 1, c, at : at + size, :],
+            )
+
+        def joined(c, at, size, last_piece):
+            got = received(c, at, size, 0)
+            for piece_r in range(1, last_piece + 1):
+                got = jnp.where(spot[0:size] < CHUNK * piece_r, got, received(c, at, size, piece_r))
+            return got
+
+        def unpack(piece_r, r0, r1, t0, t1):
+            g = [joined(c, lo, rows, piece_r) for c in range(3)]
+            gx[lo:hi, :] = g[0]
+            gx[0:lo, :] = joined(0, 0, cx, piece_r)
+            gx[hi : hi + cx, :] = joined(0, hi, cx, piece_r)
+            g_y = jnp.where(row < 4, joined(1, hi, cx, piece_r), joined(1, 0, cx, piece_r))
+            a_g = first(
+                gx[lo + 1 : hi + 1, :], gx[lo - 1 : hi - 1, :],
+                gx[lo + 2 : hi + 2, :], gx[lo - 2 : hi - 2, :],
+            )
+            g2 = g[2]
+            plus1, plus2, minus1, minus2 = turn(g2, -4), turn(g2, -8), turn(g2, 4), turn(g2, 8)
+            if t0 == 0:
+                minus1 = jnp.where(spot == 0, jnp.where(h0_here, turn(g2, -4), 0.0), minus1)
+                minus2 = jnp.where(
+                    spot == 0, jnp.where(h0_here, turn(g2, -8), 0.0),
+                    jnp.where(spot == 1, jnp.where(h0_here, g2, 0.0), minus2),
+                )
+            if t1 == nr:
+                plus1 = jnp.where(spot == nr - 1, turn(g2, half), plus1)
+                plus2 = jnp.where(
+                    spot < nr - 2, plus2,
+                    jnp.where(spot == nr - 2, turn(g2, -(half + 4)), turn(g2, -(half - 4))),
+                )
+            t_g = a_g + depth_first(plus1, minus1, plus2, minus2, jnp.where(h0_here, 1.0, -1.0))
+            for r in range(r0, r1):
+                back = (half - 2 - 4 * r) % cy
+                for c in range(3):
+                    ht[c, r] = turn(g[c], back)
+                hx[r] = turn(g_y, back)
+            for r in range(t0, t1):
+                th[r] = turn(t_g, (half - 2 - 4 * r) % cy)
 
         def reader(planes):
             def u(c, r, shift, at, size=rows):
                 return buf[par, c, pl.ds(r + 2 + shift, planes), at : at + size, :]
             return u
 
-        def prepare(b, carry):
-            u, planes = reader(PREPARE), PREPARE
-            r = b * PREPARE
+        def prepare(r, planes):
+            u = reader(planes)
             x = first(u(0, r, 0, lo + 1), u(0, r, 0, lo - 1), u(0, r, 0, lo + 2), u(0, r, 0, lo - 2))
             y = first(*along_y(u(1, r, 0, lo), ht[1, pl.ds(r, planes)], lm3))
             z = depth_first(u(2, r, 1, lo), u(2, r, -1, lo), u(2, r, 2, lo), u(2, r, -2, lo), sign)
@@ -339,10 +348,6 @@
             )
             s_ref[pl.ds(r, planes), 0:lo, :] = s_halo
             s_ref[pl.ds(r, planes), hi : hi + cx, :] = s_halo
-            return carry
-
-        lax.fori_loop(0, nr // PREPARE, prepare, 0)
-        ghosts(e_ref, (), slice(0, rows))
 
         def advance(b, carry):
             u, planes = reader(ADVANCE), ADVANCE
@@ -374,16 +379,38 @@
                 buf[place] = 2.0 * mid - buf[place] + acc
             return carry
 
-        for piece_r in range(chunks):
-            lax.fori_loop(piece_r * CHUNK // ADVANCE, (piece_r + 1) * CHUNK // ADVANCE, advance, 0)
-
+        def share(stop):
             @pl.when(n < steps - 1)
             def _():
-                send_face(new, piece_r)
-
-        @pl.when(n < steps - 1)
-        def _():
-            send_edges(new)
+                send_face(new, stop // FACE - 1)
+                if stop % CHUNK == 0:
+                    send_edges(new, stop // CHUNK - 1)
+
+        done, ready, known = 0, 0, 0
+        for piece_r in range(chunks):
+            wait_halos(par, piece_r)
+            last_piece = piece_r == chunks - 1
+            if piece_r == 0:
+                for c, span in ((0, slice(lo, hi)), (1, slice(lo, hi)), (2, slice(0, hi + cx))):
+                    ghosts(buf, (par, c), span, True)
+            if last_piece:
+                for c, span in ((0, slice(lo, hi)), (1, slice(lo, hi)), (2, slice(0, hi + cx))):
+                    ghosts(buf, (par, c), span, False)
+            upto = CHUNK * (piece_r + 1)
+            safe = nr if last_piece else upto - 2
+            unpack(piece_r, known, upto, ready, safe)
+            prepare(ready, safe - ready)
+            if piece_r == 0:
+                ghosts(e_ref, (), slice(0, rows), True)
+            if last_piece:
+                ghosts(e_ref, (), slice(0, rows), False)
+            known, ready = upto, safe
+            limit = nr if last_piece else ADVANCE * ((safe - 2) // ADVANCE)
+            while done < limit:
+                stop = done + FACE
+                lax.fori_loop(done // ADVANCE, stop // ADVANCE, advance, 0)
+                share(stop)
+                done = stop
 
     def surface_copy(moment, par, da, dg):
         to_a, to_g = lax.rem(a + da, 2), lax.rem(gy + dg, gys)
@@ -460,8 +487,11 @@
 
         @pl.when(stage == 0)
         def _():
+            span = pl.ds(pl.multiple_of(group * UNIT, UNIT), UNIT)
+            rows_of = [force[c, span, :] for c in range(3)]
             for i in range(UNIT):
-                vs[i, 0:3, :] = force[group * UNIT + i] * (1.0 / SCALE)
+                for c in range(3):
+                    vs[i, c : c + 1, :] = rows_of[c][i : i + 1] * (1.0 / SCALE)
 
         v = [vs[i] for i in range(UNIT)]
         total = list(v)
@@ -485,26 +515,23 @@
                         result[c : c + 1, 128 * h : 128 * (h + 1)]
                     )
 
-    def tick(i):
-        @pl.when(i < units)
-        def _():
-            respond(i)
-            for dk in range(1, pairs):
-                spread(i, dk).start()
-
-        for phase in range(4):
-            unit = i - 1 - phase
+    def tick_links(i):
+        for phase in range(5):
+            unit = i - 1 - 2 * phase
 
             @pl.when((unit >= 0) & (unit < units))
             def _():
+                if phase == 1:
+                    for dk in range(1, pairs):
+                        spread(unit, dk).wait_recv()
+                elif phase > 1:
+                    for leg in LEGS[phase - 2]:
+                        hop(unit, leg).wait_recv()
                 if phase == 0:
                     for dk in range(1, pairs):
-                        spread(unit, dk).wait_recv()
-                else:
+                        spread(unit, dk).start()
+                elif phase < 4:
                     for leg in LEGS[phase - 1]:
-                        hop(unit, leg).wait_recv()
-                if phase < 3:
-                    for leg in LEGS[phase]:
                         hop(unit, leg).start()
 
     def body(i, carry):
@@ -515,9 +542,10 @@
         def _():
             for j in range(8):
                 give(j).wait()
+            for part in range(nr // FACE):
+                send_face(0, part)
             for piece_r in range(chunks):
-                send_face(0, piece_r)
-            send_edges(0)
+                send_edges(0, piece_r)
 
         @pl.when(n >= 0)
         def _():
@@ -527,7 +555,11 @@
         def _():
             send_surface(lax.div(n, EVERY), 1 - par)
 
-        tick(i)
+        tick_links(i)
+
+        @pl.when(i < units)
+        def _():
+            respond(i)
 
         @pl.when((n > 0) & (lax.rem(n + EARLY * EVERY, EVERY) == EVERY - 1) & (n < steps - 1))
         def _():
@@ -616,13 +648,13 @@
         scratch_shapes=[
             vmem((8, nz, cx, cy), f32),
             vmem((arch, width, width), jnp.bfloat16),
-            vmem((arch, 3, width), f32),
+            vmem((3, arch, width), f32),
             vmem((8, nr, cx, cy), f32),
             vmem((2, 3, nr + 4, tall, cy), f32),
             vmem((nr, rows, cy), f32),
             vmem((nr, rows, cy), f32),
-            vmem((2, 3, rows, cy), f32),
-            vmem((2, 2, 3, tall, cy), f32),
+            vmem((2, chunks, 3, rows, cy), f32),
+            vmem((2, chunks, 2, 3, tall, cy), f32),
             vmem((tall, cy), f32),
             vmem((3, nr, rows, cy), f32),
             vmem((nr, rows, cy), f32),
@@ -641,10 +673,10 @@
             dma((6,)),
             dma((8,)),
             dma((8,)),
-            dma((2, 2, chunks)),
-            dma((2, 2, chunks)),
-            dma((2, 8)),
-            dma((2, 8)),
+            dma((2, 2, nr // FACE)),
+            dma((2, 2, nr // FACE)),
+            dma((2, chunks, 8)),
+            dma((2, chunks, 8)),
             dma((units, pairs - 1)),
             dma((units, pairs - 1)),
             dma((units, 5)),
@@ -659,7 +691,7 @@
         ),
     )(
         displacement, previous, shear_coef, bulk_coef, cell_index.reshape(1, count),
-        archetype_id[:, 0], transition, forcing,
+        archetype_id[:, 0], transition, forcing.transpose(1, 0, 2),
     )
 
 

time: 153 us -> 145 us (0.948)
  Pallas kernels: 147 us -> 140 us
  local copies, waits for them, and re-layouts: 5.65 us -> 4.03 us
    pallas_call x1, Pallas kernels: 147 us -> 140 us  [per_device(): pl.pallas_call(city_kernel, out_shape=(jax.ShapeDtypeStruct(displacement....]
    unnamed x3 -> x2, local copies, waits for them, and re-layouts: 5.65 us -> 4.03 us
where the time goes in v3:
time: 145 us
  Pallas kernels  140 us (97%)
  local copies, waits for them, and re-layouts  4.03 us (3%)
    pallas_call x1, Pallas kernels, per_device(): pl.pallas_call(city_kernel, out_shape=(jax.ShapeDtypeStruct(displacement....  140 us
    unnamed x2, local copies, waits for them, and re-layouts  4.03 us

profile of v3, /device:TPU:0, one launch (start us, length us, event | category | flops | bytes accessed | tf_op | source)
XLA Modules:
  0.0 144.9 jit_solution(9866756256348331786)
XLA Ops:
  0.6 140.2 %shard_map.95 = (f32[3,32,8,128]{3,2,1,0:T(8,128)}, f32[1024,256]{1,0:T(8,128)}) custom-call(f32[3,32,8,128]{3,2,1,0:T(8,128)} %d_hbm.1, f32[3,32,8,128]{3,2,1,0:T(8,128)} %p_hbm.1, f32[32,8,128]{2,1,0:T(8,128)} %sh_hbm.1, f32[32,8,128]{2,1,0:T(8,128)} %bk_hbm.1, s32[1,1024]{1,0:T(1,128)} %bitcast.4, s32[1024]{0:T(1024)} %bitcast.5, ...), custom_call_target="tpu_custom_call" | custom-call | tf_op jit(solution)/shard_map/pallas_call | solution.py:640
  140.8 1.8 %copy.12 = f32[3,32,8,128]{3,2,1,0:T(8,128)} copy(f32[3,32,8,128]{3,2,1,0:T(8,128)} %get-tuple-element.4) | data formatting | bytes 786432
  142.6 2.3 %copy.13 = f32[1024,256]{1,0:T(8,128)} copy(f32[1024,256]{1,0:T(8,128)} %get-tuple-element.5) | data formatting | bytes 2097152

commit v4 on v3

--- a/solution.py
+++ b/solution.py
@@ -25,7 +25,7 @@
 
 
 def first(plus1, minus1, plus2, minus2):
-    return B1 * (plus1 - minus1) + B2 * (plus2 - minus2)
+    return (plus2 - minus2) + (B1 / B2) * (plus1 - minus1)
 
 
 def city_kernel(
@@ -151,6 +151,8 @@
             loads[{0: 0, 3: 1, 6: 2, 7: 3}[i]].wait()
         for r in range(nr):
             near, far = raw[i, r], raw[i, nz - 1 - r]
+            if i >= 6:
+                near, far = near * A2, far * A2
             lower, upper = folded(near, far, False), folded(near, far, True)
             kept_ref(i, r)[...] = jnp.where(hsel == 0, lower, upper)
             sbuf[i, r] = jnp.where(hsel == 0, upper, lower)
@@ -253,7 +255,7 @@
     lm1 = lax.rem(lane, half)[None]
 
     def depth_first(plus1, minus1, plus2, minus2, sgn):
-        return (B1 * sgn) * (plus1 - minus1) + (B2 * sgn) * (plus2 - minus2)
+        return sgn * ((plus2 - minus2) + (B1 / B2) * (plus1 - minus1))
 
     def along_y(core, halo, lm):
         return (
@@ -366,15 +368,15 @@
                 y = along_y(mid, ht[c, pl.ds(r, planes)], lm3)
                 near = [u(c, r, 0, lo + 1) + u(c, r, 0, lo - 1), y[0] + y[1], u(c, r, 1, lo) + u(c, r, -1, lo)]
                 far = [u(c, r, 0, lo + 2) + u(c, r, 0, lo - 2), y[2] + y[3], u(c, r, 2, lo) + u(c, r, -2, lo)]
-                lap = (3.0 * A0) * mid + A1 * (near[0] + near[1] + near[2]) + A2 * (far[0] + far[1] + far[2])
-                own_second = A0 * mid + A1 * near[c] + A2 * far[c]
+                lap = (3.0 * A0 / A2) * mid + (A1 / A2) * (near[0] + near[1] + near[2]) + (far[0] + far[1] + far[2])
+                own_second = (A0 / A2) * mid + (A1 / A2) * near[c] + far[c]
                 if c == 0:
                     cross = first(s(lo + 1), s(lo - 1), s(lo + 2), s(lo - 2))
                 elif c == 1:
                     cross = first(*along_y(q_ref[pl.ds(r, planes)], th[pl.ds(r, planes)], lm3))
                 else:
                     cross = depth_first(e(1), e(-1), e(2), e(-2), sign)
-                acc = sh * lap + bk * (own_second + cross)
+                acc = sh * lap + bk * (own_second + (B2 * B2 / A2) * cross)
                 place = (new, c, pl.ds(r + 2, planes), slice(lo, hi), slice(None))
                 buf[place] = 2.0 * mid - buf[place] + acc
             return carry
@@ -410,6 +412,10 @@
                 stop = done + FACE
                 lax.fori_loop(done // ADVANCE, stop // ADVANCE, advance, 0)
                 share(stop)
+                if stop == FACE:
+                    @pl.when(lax.rem(n, EVERY) == EVERY - 1)
+                    def _():
+                        send_surface(lax.div(n, EVERY), new)
                 done = stop
 
     def surface_copy(moment, par, da, dg):
@@ -551,15 +557,11 @@
         def _():
             grid_step(n, par)
 
-        @pl.when((n >= 0) & (lax.rem(n + EARLY * EVERY, EVERY) == EVERY - 1))
-        def _():
-            send_surface(lax.div(n, EVERY), 1 - par)
-
-        tick_links(i)
-
         @pl.when(i < units)
         def _():
             respond(i)
+
+        tick_links(i)
 
         @pl.when((n > 0) & (lax.rem(n + EARLY * EVERY, EVERY) == EVERY - 1) & (n < steps - 1))
         def _():

time: 145 us -> 140 us (0.966)
  Pallas kernels: 140 us -> 135 us
    pallas_call x1, Pallas kernels: 140 us -> 135 us  [per_device(): pl.pallas_call(city_kernel, out_shape=(jax.ShapeDtypeStruct(displacement....]
where the time goes in v4:
time: 140 us
  Pallas kernels  135 us (96%)
  local copies, waits for them, and re-layouts  4.03 us (3%)
    pallas_call x1, Pallas kernels, per_device(): pl.pallas_call(city_kernel, out_shape=(jax.ShapeDtypeStruct(displacement....  135 us
    unnamed x2, local copies, waits for them, and re-layouts  4.03 us

profile of v4, /device:TPU:0, one launch (start us, length us, event | category | flops | bytes accessed | tf_op | source)
XLA Modules:
  0.0 139.5 jit_solution(9491248644413063970)
XLA Ops:
  0.6 134.8 %shard_map.95 = (f32[3,32,8,128]{3,2,1,0:T(8,128)}, f32[1024,256]{1,0:T(8,128)}) custom-call(f32[3,32,8,128]{3,2,1,0:T(8,128)} %d_hbm.1, f32[3,32,8,128]{3,2,1,0:T(8,128)} %p_hbm.1, f32[32,8,128]{2,1,0:T(8,128)} %sh_hbm.1, f32[32,8,128]{2,1,0:T(8,128)} %bk_hbm.1, s32[1,1024]{1,0:T(1,128)} %bitcast.4, s32[1024]{0:T(1024)} %bitcast.5, ...), custom_call_target="tpu_custom_call" | custom-call | tf_op jit(solution)/shard_map/pallas_call | solution.py:642
  135.5 1.8 %copy.12 = f32[3,32,8,128]{3,2,1,0:T(8,128)} copy(f32[3,32,8,128]{3,2,1,0:T(8,128)} %get-tuple-element.4) | data formatting | bytes 786432
  137.3 2.3 %copy.13 = f32[1024,256]{1,0:T(8,128)} copy(f32[1024,256]{1,0:T(8,128)} %get-tuple-element.5) | data formatting | bytes 2097152
